TPU v7x, 32 devices: a whole 2x2x4 slice. The times are simulated.
32 devices in a mesh: facet: 8 (over z, x), col: 4 (over y, core).
Axes of the slice: x: 2, y: 2, z: 4, core: 2. Of those that a mesh axis runs over, the one named last changes fastest.
Arguments:
- facets: bfloat16 [2, 8192, 1024], P(None, ('facet', 'col')), may hold values from -6 to 6
- observed: float32 [2, 32, 1024], P(None, 'col'), may hold values from -6 to 6
- uv_cells: int32 [2, 32, 1024], P(None, 'col'), may hold values from 0 to 511
- counts: int32 [32], P('col'), may hold values from 64 to 1024, as said below
Outputs:
- facet_residual: float32 [2, 8192, 1024], P(None, ('facet', 'col'))
Inputs may be any that keep to these rules, and one draw needn't show every extreme that they name: Live slots of a subgrid are its first counts[s] slots; in every column some subgrid has all 1024 slots live.
All inputs are finite; a program needn't handle non-finite values.
Results may differ from a plain program's by a relative error of at most 0.008.
Values may be sent and summed in bfloat16 or wider, within the bound.
A program may use at most 64 MiB of HBM per device.

v0:
```python
import functools
import math

import jax
import jax.numpy as jnp
import numpy as np
from jax import lax
from jax.experimental import pallas as pl
from jax.experimental.pallas import tpu as pltpu
from jax.sharding import PartitionSpec as P

S = 512
IMAGE = 65536
MESH = pl.DeviceIdType.MESH
BF = jnp.bfloat16
F32 = jnp.float32


def unit(ticks):
    angle = (np.asarray(ticks, np.int64) % IMAGE) * (-2.0 * math.pi / IMAGE)
    return np.cos(angle), np.sin(angle)


def make_constants(facets, columns, per_column, extent):
    window = S // 8
    spacing = IMAGE // extent
    parts = window // 16
    cells = np.arange(extent, dtype=np.int64)
    weight = (0.6 + 0.4 * np.sin(math.pi * (cells + 0.5) / extent) ** 2) / math.sqrt(extent)
    low = np.arange(16, dtype=np.int64)
    high = 16 * np.arange(parts, dtype=np.int64)
    col = np.arange(columns, dtype=np.int64)
    vc = col * (IMAGE // 4) + (29 * col + 3) % spacing
    sub = np.arange(per_column, dtype=np.int64)
    us = sub * (IMAGE // 64) + (37 * sub + 5) % (IMAGE * 8 // S)
    grain = IMAGE // window
    rows = []
    for ticks, scale in (
        (spacing * low[:, None] * cells, 1.0),
        ((vc[:, None] + spacing * high).reshape(-1, 1) * cells, weight),
        (grain * low[:, None] * cells, 1.0),
        ((us[:, None] + grain * high).reshape(-1, 1) * cells, weight),
    ):
        real, imag = unit(ticks)
        rows += [real * scale, imag * scale]
    groups = max(facets // 8, 1)
    wide = max(columns, per_column)
    scalars = np.zeros((8 + groups, 2 * wide))
    for index in range(8):
        real, imag = unit(index * extent * vc)
        scalars[index, :columns] = real
        scalars[index, wide : wide + columns] = imag
    for index in range(groups):
        real, imag = unit(index * extent * us)
        scalars[8 + index, :per_column] = real
        scalars[8 + index, wide : wide + per_column] = imag
    return np.concatenate(rows).astype(np.float32), scalars.astype(np.float32)


def spin(value, first, second):
    half = value.shape[1] // 2
    lane = lax.broadcasted_iota(jnp.int32, value.shape, 1)
    return pltpu.roll(value, half, 1) * jnp.where(lane < half, first, second)


def cycle_kernel(
    nf, nc, x_hbm, obs, cells, counts, con, scal, back_out, tab_out,
    xbuf, tab, t2, tt, s_send, s_recv, g_send, g_recv, lt, rtr, rti, r1r, r1i, wt,
    r_send, r_recv, b_send, b_recv,
    x_sem, o_sem, sa, ra, sb, rb, sc, rc, sd, rd,
):
    f = lax.axis_index("facet")
    c = lax.axis_index("col")
    window = S // 8
    two = 2 * window
    parts = window // 16
    pc = nf
    rows = xbuf.shape[1]
    groups = max(nf // 8, 1)
    wide = max(nc, pc)
    vis = obs.shape[2]
    col_order = [d for d in range(nc - 1, 0, -1)]
    facet_order = sorted(range(1, nf), key=lambda d: -min(d, nf - d))

    barrier = pltpu.get_barrier_semaphore()
    for d in range(1, nc):
        pl.semaphore_signal(barrier, inc=1, device_id=(f, lax.rem(c + d, nc)), device_id_type=MESH)
    for d in range(1, nf):
        pl.semaphore_signal(barrier, inc=1, device_id=(lax.rem(f + d, nf), c), device_id_type=MESH)

    x_copy = pltpu.make_async_copy(x_hbm, xbuf, x_sem)
    x_copy.start()

    e1 = 32
    f0 = e1 + 2 * nc * parts
    h0 = f0 + 32
    fm = lax.rem(f, 8)

    def col_body(i, carry):
        ci = i // parts
        li = i - ci * parts
        pr, pi = scal[fm, ci], scal[fm, wide + ci]
        ar, ai = con[pl.ds(e1 + i, 1), :], con[pl.ds(e1 + nc * parts + i, 1), :]
        er, ei = ar * pr - ai * pi, ar * pi + ai * pr
        lr, lm = con[0:16, :], con[16:32, :]
        real = (lr * er - lm * ei).astype(BF)
        imag = (lr * ei + lm * er).astype(BF)
        top = pl.multiple_of(ci * two + li * 16, 16)
        low = pl.multiple_of(ci * two + window + li * 16, 16)
        tab[0, pl.ds(top, 16), :] = real
        tab[0, pl.ds(low, 16), :] = imag
        tab[1, pl.ds(top, 16), :] = -imag
        tab[1, pl.ds(low, 16), :] = real
        return carry

    lax.fori_loop(0, nc * parts, col_body, 0)
    o_copy = pltpu.make_async_copy(tab, tab_out, o_sem)
    o_copy.start()
    x_copy.wait()
    nt = (((1,), (1,)), ((), ()))
    strip = lax.dot_general(xbuf[0], tab[0], nt, preferred_element_type=F32)
    strip += lax.dot_general(xbuf[1], tab[1], nt, preferred_element_type=F32)
    for k in range(nc):
        s_send[k] = strip[:, k * two : (k + 1) * two].astype(BF)
    pl.semaphore_wait(barrier, nc - 1 + nf - 1)

    def a_copy(d):
        peer, src = lax.rem(c + d, nc), lax.rem(c + nc - d, nc)
        out = pltpu.make_async_remote_copy(
            s_send.at[peer], s_recv.at[c], sa.at[peer], ra.at[c], (f, peer), MESH
        )
        arrive = pltpu.make_async_remote_copy(
            s_send.at[peer], s_recv.at[src], sa.at[peer], ra.at[src], (f, peer), MESH
        )
        return out, arrive, src

    sends = []
    for d in col_order:
        out = a_copy(d)[0]
        out.start()
        sends.append(out)

    half = pc * window
    fg = f // 8

    def row_body(i, carry):
        j = i // parts
        ki = i - j * parts
        pr, pi = scal[8 + fg, j], scal[8 + fg, wide + j]
        ar, ai = con[pl.ds(h0 + i, 1), :], con[pl.ds(h0 + pc * parts + i, 1), :]
        er, ei = ar * pr - ai * pi, ar * pi + ai * pr
        lr, lm = con[f0 : f0 + 16, :], con[f0 + 16 : f0 + 32, :]
        at = pl.multiple_of(j * window + ki * 16, 16)
        t2[pl.ds(at, 16), :] = (lr * er - lm * ei).astype(BF)
        t2[pl.ds(pl.multiple_of(half + at, 16), 16), :] = (lr * ei + lm * er).astype(BF)
        return carry

    lax.fori_loop(0, pc * parts, row_body, 0)

    def part_product(src, block):
        start = pl.multiple_of(src * rows, rows)
        return jnp.dot(t2[:, pl.ds(start, rows)], block, preferred_element_type=F32)

    acc = part_product(c, s_send[c])
    for d in col_order[::-1]:
        unused, arrive, src = a_copy(d)
        arrive.wait_recv()
        acc += part_product(src, s_recv[src])
    win = (acc[:half] + spin(acc[half:], -1.0, 1.0)).astype(BF)
    for j in range(pc):
        g_send[j] = win[j * window : (j + 1) * window]

    def b_copy(d):
        peer, src = lax.rem(f + d, nf), lax.rem(f + nf - d, nf)
        out = pltpu.make_async_remote_copy(
            g_send.at[peer], g_recv.at[f], sb.at[peer], rb.at[f], (peer, c), MESH
        )
        arrive = pltpu.make_async_remote_copy(
            g_send.at[peer], g_recv.at[src], sb.at[peer], rb.at[src], (peer, c), MESH
        )
        return out, arrive

    for d in facet_order:
        out = b_copy(d)[0]
        out.start()
        sends.append(out)
    g_recv[f] = g_send[f]

    first = cells[0, pl.ds(f, 1), :]
    second = cells[1, pl.ds(f, 1), :]

    def wave(count, step, cell):
        index = step * lax.broadcasted_iota(jnp.int32, (count, vis), 0)
        angle = (index * cell & (S - 1)).astype(F32) * (-2.0 * math.pi / S)
        return jnp.cos(angle), jnp.sin(angle)

    l0r, l0i = wave(16, 1, first)
    l1r, l1i = wave(max(groups * parts, 8), 16, first)
    for i in range(groups * parts):
        er, ei = l1r[i : i + 1], l1i[i : i + 1]
        g, k = i // parts, i % parts
        at = g * two + k * 16
        lt[at : at + 16, :] = (l0r * er - l0i * ei).astype(BF)
        lt[at + window : at + window + 16, :] = (l0r * ei + l0i * er).astype(BF)
    m0r, m0i = wave(16, 1, second)
    r1r[...], r1i[...] = wave(S // 16, 16, second)

    def right_body(i, carry):
        er, ei = r1r[pl.ds(i, 1), :], r1i[pl.ds(i, 1), :]
        at = pl.multiple_of(i * 16, 16)
        rtr[pl.ds(at, 16), :] = m0r * er - m0i * ei
        rti[pl.ds(at, 16), :] = m0r * ei + m0i * er
        return carry

    lax.fori_loop(0, S // 16, right_body, 0)
    for i in range(2 * half // 256):
        tt[:, i * 256 : (i + 1) * 256] = t2[i * 256 : (i + 1) * 256, :].T

    for d in facet_order:
        b_copy(d)[1].wait_recv()

    pred_r = jnp.zeros((8, vis), F32)
    pred_i = jnp.zeros((8, vis), F32)
    for b in range(8):
        inner = None
        for g in range(groups):
            block = g_recv[g * 8 + b].astype(F32)
            both = jnp.concatenate([block, spin(block, -1.0, 1.0)], axis=0)
            term = jnp.dot(
                both.T.astype(BF), lt[g * two : (g + 1) * two, :], preferred_element_type=F32
            )
            inner = term if inner is None else inner + term
        ir, ii = inner[:window], inner[window:]
        rr, ri = rtr[b * window : (b + 1) * window, :], rti[b * window : (b + 1) * window, :]
        pred_r += jnp.sum((ir * rr - ii * ri).reshape(window // 8, 8, vis), axis=0)
        pred_i += jnp.sum((ir * ri + ii * rr).reshape(window // 8, 8, vis), axis=0)
    live = lax.broadcasted_iota(jnp.int32, (1, vis), 1) < counts[f]
    res_r = jnp.where(
        live, obs[0, pl.ds(f, 1), :] - jnp.sum(pred_r, axis=0, keepdims=True) / S, 0.0
    )
    res_i = jnp.where(
        live, obs[1, pl.ds(f, 1), :] - jnp.sum(pred_i, axis=0, keepdims=True) / S, 0.0
    )

    def c_copy(peer, src):
        out = pltpu.make_async_remote_copy(
            r_send.at[peer], r_recv.at[f], sc.at[peer], rc.at[f], (peer, c), MESH
        )
        arrive = pltpu.make_async_remote_copy(
            r_send.at[peer], r_recv.at[src], sc.at[peer], rc.at[src], (peer, c), MESH
        )
        return out, arrive

    scale = 1.0 / math.sqrt(vis)
    for b in range(0, 8, 2):
        for h in range(2):
            at = (b + h) * window
            rr, ri = rtr[at : at + window, :], rti[at : at + window, :]
            wt[2 * at : 2 * at + window, :] = (res_r * rr + res_i * ri).astype(BF)
            wt[2 * at + window : 2 * at + two, :] = (res_i * rr - res_r * ri).astype(BF)
        grid = lax.dot_general(
            lt[...], wt[b * two : (b + 2) * two, :], nt, preferred_element_type=F32
        )
        for g in range(groups):
            for h in range(2):
                u = grid[g * two : g * two + window, h * two : (h + 1) * two]
                v = grid[g * two + window : (g + 1) * two, h * two : (h + 1) * two]
                r_send[g * 8 + b + h] = ((u + spin(v, 1.0, -1.0)) * scale).astype(BF)
    for d in facet_order:
        out = c_copy(lax.rem(f + d, nf), lax.rem(f + nf - d, nf))[0]
        out.start()
        sends.append(out)
    r_recv[f] = r_send[f]
    for d in facet_order:
        c_copy(lax.rem(f + d, nf), lax.rem(f + nf - d, nf))[1].wait_recv()

    ret = r_recv[...].reshape(half, two)
    other = spin(ret.astype(F32), 1.0, -1.0).astype(BF)
    strip = jnp.dot(tt[:, :half], ret, preferred_element_type=F32)
    strip += jnp.dot(tt[:, half:], other, preferred_element_type=F32)
    for k in range(nc):
        b_send[k] = strip[k * rows : (k + 1) * rows].astype(BF)

    def d_copy(d):
        peer, src = lax.rem(c + d, nc), lax.rem(c + nc - d, nc)
        out = pltpu.make_async_remote_copy(
            b_send.at[peer], b_recv.at[c], sd.at[peer], rd.at[c], (f, peer), MESH
        )
        arrive = pltpu.make_async_remote_copy(
            b_send.at[peer], b_recv.at[src], sd.at[peer], rd.at[src], (f, peer), MESH
        )
        return out, arrive

    for d in col_order:
        out = d_copy(d)[0]
        out.start()
        sends.append(out)
    b_recv[c] = b_send[c]
    o_copy.wait()
    for d in col_order:
        d_copy(d)[1].wait_recv()
    back_out[...] = b_recv[...]
    for out in sends:
        out.wait_send()


def image_kernel(nc, back, tab, out):
    strip = jnp.concatenate([back[k] for k in range(nc)], axis=1)
    out[0] = jnp.dot(strip, tab[0], preferred_element_type=F32)
    out[1] = jnp.dot(strip, tab[1], preferred_element_type=F32)


def solution(mesh):
    nf, nc = mesh.shape["facet"], mesh.shape["col"]

    def on_device(facets, observed, uv_cells, counts):
        rows, extent = facets.shape[1:]
        vis = observed.shape[2]
        pc = counts.shape[0]
        window = S // 8
        two = 2 * window
        groups = nf // 8
        assert pc == nf and nf % 8 == 0 and nf <= 32
        con, scal = make_constants(nf, nc, pc, extent)
        vmem = pl.BlockSpec(memory_space=pltpu.VMEM)
        smem = pl.BlockSpec(memory_space=pltpu.SMEM)
        hbm = pl.BlockSpec(memory_space=pl.ANY)
        dma = pltpu.SemaphoreType.DMA
        back, tab = pl.pallas_call(
            functools.partial(cycle_kernel, nf, nc),
            out_shape=(
                jax.ShapeDtypeStruct((nc, rows, two), BF),
                jax.ShapeDtypeStruct((2, nc * two, extent), BF),
            ),
            in_specs=[hbm, vmem, vmem, smem, vmem, smem],
            out_specs=(vmem, hbm),
            scratch_shapes=[
                pltpu.VMEM((2, rows, extent), BF),
                pltpu.VMEM((2, nc * two, extent), BF),
                pltpu.VMEM((2 * pc * window, extent), BF),
                pltpu.VMEM((extent, 2 * pc * window), BF),
                pltpu.VMEM((nc, rows, two), BF),
                pltpu.VMEM((nc, rows, two), BF),
                pltpu.VMEM((pc, window, two), BF),
                pltpu.VMEM((nf, window, two), BF),
                pltpu.VMEM((groups * two, vis), BF),
                pltpu.VMEM((S, vis), F32),
                pltpu.VMEM((S, vis), F32),
                pltpu.VMEM((S // 16, vis), F32),
                pltpu.VMEM((S // 16, vis), F32),
                pltpu.VMEM((2 * S, vis), BF),
                pltpu.VMEM((nf, window, two), BF),
                pltpu.VMEM((pc, window, two), BF),
                pltpu.VMEM((nc, rows, two), BF),
                pltpu.VMEM((nc, rows, two), BF),
                dma, dma,
                dma((nc,)), dma((nc,)), dma((nf,)), dma((nf,)),
                dma((nf,)), dma((nf,)), dma((nc,)), dma((nc,)),
            ],
            compiler_params=pltpu.CompilerParams(collective_id=0, has_side_effects=True),
            name="cycle",
        )(facets, observed, uv_cells, counts, jnp.asarray(con), jnp.asarray(scal))
        tile = 256
        return pl.pallas_call(
            functools.partial(image_kernel, nc),
            grid=(extent // tile,),
            out_shape=jax.ShapeDtypeStruct((2, rows, extent), F32),
            in_specs=[
                pl.BlockSpec((nc, rows, two), lambda i: (0, 0, 0)),
                pl.BlockSpec((2, nc * two, tile), lambda i: (0, 0, i)),
            ],
            out_specs=pl.BlockSpec((2, rows, tile), lambda i: (0, 0, i)),
            name="image",
        )(back, tab)

    return jax.shard_map(
        on_device,
        mesh=mesh,
        in_specs=(
            P(None, ("facet", "col"), None),
            P(None, "col", None),
            P(None, "col", None),
            P("col"),
        ),
        out_specs=P(None, ("facet", "col"), None),
        check_vma=False,
    )
```

profile of v0, /device:TPU:0, one launch (start us, length us, event | category | flops | bytes accessed | tf_op | source)
XLA Modules:
  0.0 35.1 jit_solution(4290096101739768331)
XLA Ops:
  0.0 30.7 %cycle.1 = (bf16[4,256,128]{2,1,0:T(8,128)(2,1)}, bf16[2,512,1024]{2,1,0:T(8,128)(2,1)}) custom-call(bf16[2,256,1024]{2,1,0:T(8,128)(2,1)} %x_hbm.1, f32[2,8,1024]{2,1,0:T(8,128)} %obs.1, s32[2,8,1024]{2,1,0:T(8,128)} %cells.1, s32[8]{0:T(128)} %counts.1, f32[160,1024]{1,0:T(8,128)} %constant.4.clone.con, f32[9,16]{1,0:T(8,128)} %constant.5.clone.scal), custom_call_target="tpu_custom_call" | custom-call | tf_op jit(solution)/shard_map/cycle/pallas_call | solution.py:329
  30.7 4.4 %image.1 = f32[2,256,1024]{2,1,0:T(8,128)} custom-call(bf16[4,256,128]{2,1,0:T(8,128)(2,1)} %get-tuple-element.7.back, bf16[2,512,1024]{2,1,0:T(8,128)(2,1)} %get-tuple-element.8.tab), custom_call_target="tpu_custom_call" | custom-call | tf_op jit(solution)/shard_map/image/pallas_call | solution.py:364
where the time goes:
time: 35.3 us; the launch traced here: 35.1 us
  Pallas kernels  35.1 us (99%)
    pallas_call x1, Pallas kernels, on_device(): pl.pallas_call(functools.partial(cycle_kernel, nf, nc), out_shape=(jax.Sh...  30.7 us
    pallas_call x1, Pallas kernels, on_device(): pl.pallas_call(functools.partial(image_kernel, nc), grid=(extent // tile,...  4.4 us

commit v1 on v0

v1 whole, which is shorter than its diff:
```python
import functools
import math

import jax
import jax.numpy as jnp
import numpy as np
from jax import lax
from jax.experimental import pallas as pl
from jax.experimental.pallas import tpu as pltpu
from jax.sharding import PartitionSpec as P

S = 512
IMAGE = 65536
MESH = pl.DeviceIdType.MESH
BF = jnp.bfloat16
F32 = jnp.float32


def unit(ticks):
    angle = (np.asarray(ticks, np.int64) % IMAGE) * (-2.0 * math.pi / IMAGE)
    return np.cos(angle), np.sin(angle)


def make_constants(facets, columns, per_column, extent):
    window = S // 8
    spacing = IMAGE // extent
    parts = window // 16
    cells = np.arange(extent, dtype=np.int64)
    weight = (0.6 + 0.4 * np.sin(math.pi * (cells + 0.5) / extent) ** 2) / math.sqrt(extent)
    low = np.arange(16, dtype=np.int64)
    high = 16 * np.arange(parts, dtype=np.int64)
    col = np.arange(columns, dtype=np.int64)
    vc = col * (IMAGE // 4) + (29 * col + 3) % spacing
    sub = np.arange(per_column, dtype=np.int64)
    us = sub * (IMAGE // 64) + (37 * sub + 5) % (IMAGE * 8 // S)
    grain = IMAGE // window
    rows = []
    for ticks, scale in (
        (spacing * low[:, None] * cells, 1.0),
        ((vc[:, None] + spacing * high).reshape(-1, 1) * cells, weight),
        (grain * low[:, None] * cells, 1.0),
        ((us[:, None] + grain * high).reshape(-1, 1) * cells, weight),
    ):
        real, imag = unit(ticks)
        rows += [real * scale, imag * scale]
    groups = max(facets // 8, 1)
    wide = max(columns, per_column)
    scalars = np.zeros((8 + groups, 2 * wide))
    for index in range(8):
        real, imag = unit(index * extent * vc)
        scalars[index, :columns] = real
        scalars[index, wide : wide + columns] = imag
    for index in range(groups):
        real, imag = unit(index * extent * us)
        scalars[8 + index, :per_column] = real
        scalars[8 + index, wide : wide + per_column] = imag
    return np.concatenate(rows).astype(np.float32), scalars.astype(np.float32)


def spin(value, first, second):
    half = value.shape[1] // 2
    lane = lax.broadcasted_iota(jnp.int32, value.shape, 1)
    return pltpu.roll(value, half, 1) * jnp.where(lane < half, first, second)


def cycle_kernel(
    nf, nc, xbuf, obs, cells, counts, con, scal, back_out, tab,
    t2, tt, s_send, s_recv, g_send, g_recv, lt, rtr, rti, r1r, r1i, wt,
    r_send, r_recv, b_send, b_recv,
    sa, ra, sb, rb, sc, rc, sd, rd,
):
    f = lax.axis_index("facet")
    c = lax.axis_index("col")
    window = S // 8
    two = 2 * window
    parts = window // 16
    pc = nf
    rows = xbuf.shape[1]
    groups = nf // 8
    wide = max(nc, pc)
    vis = obs.shape[2]
    if nc % 2:
        col_steps = [(d, 0) for d in range(1, nc)]
    else:
        col_steps = [(d, k) for d in range(nc // 2 - 1, -1, -1) for k in range(2) if d or k]

    def col_at(step, sign):
        if nc % 2:
            return lax.rem(c + nc + sign * step[0], nc)
        top = lax.rem(c // 2 + nc // 2 + sign * step[0], nc // 2)
        return 2 * top + lax.rem(c + step[1], 2)

    def pair_at(q):
        return lax.rem(f // 2 + q, 4)

    def facet_link(src_buf, dst_buf, send, recv, peer, slot):
        return pltpu.make_async_remote_copy(
            src_buf.at[peer], dst_buf.at[slot], send.at[peer], recv.at[slot], (peer, c), MESH
        )

    def col_link(src_buf, dst_buf, send, recv, peer, slot):
        return pltpu.make_async_remote_copy(
            src_buf.at[peer], dst_buf.at[slot], send.at[peer], recv.at[slot], (f, peer), MESH
        )

    barrier = pltpu.get_barrier_semaphore()
    for d in range(1, nc):
        pl.semaphore_signal(barrier, inc=1, device_id=(f, lax.rem(c + d, nc)), device_id_type=MESH)
    for d in range(1, nf):
        pl.semaphore_signal(barrier, inc=1, device_id=(lax.rem(f + d, nf), c), device_id_type=MESH)

    e1 = 32
    f0 = e1 + 2 * nc * parts
    h0 = f0 + 32
    nt = (((1,), (1,)), ((), ()))
    fm = lax.rem(f, 8)

    def column_table(cp):
        pr, pi = scal[fm, cp], scal[fm, wide + cp]
        lr, lm = con[0:16, :], con[16:32, :]
        for li in range(parts):
            i = cp * parts + li
            ar, ai = con[pl.ds(e1 + i, 1), :], con[pl.ds(e1 + nc * parts + i, 1), :]
            er, ei = ar * pr - ai * pi, ar * pi + ai * pr
            real = (lr * er - lm * ei).astype(BF)
            imag = (lr * ei + lm * er).astype(BF)
            top = pl.multiple_of(cp * two + li * 16, 16)
            low = pl.multiple_of(cp * two + window + li * 16, 16)
            tab[0, pl.ds(top, 16), :] = real
            tab[0, pl.ds(low, 16), :] = imag
            tab[1, pl.ds(top, 16), :] = -imag
            tab[1, pl.ds(low, 16), :] = real

    def column_strip(cp):
        at = pl.multiple_of(cp * two, two)
        strip = lax.dot_general(xbuf[0], tab[0, pl.ds(at, two), :], nt, preferred_element_type=F32)
        strip += lax.dot_general(xbuf[1], tab[1, pl.ds(at, two), :], nt, preferred_element_type=F32)
        s_send[cp] = strip.astype(BF)

    for n, step in enumerate(col_steps):
        peer = col_at(step, 1)
        column_table(peer)
        column_strip(peer)
        if n == 0:
            pl.semaphore_wait(barrier, nc - 1 + nf - 1)
        col_link(s_send, s_recv, sa, ra, peer, c).start()
    column_table(c)
    column_strip(c)

    half = pc * window
    fg = f // 8

    def row_body(i, carry):
        j = i // parts
        ki = i - j * parts
        pr, pi = scal[8 + fg, j], scal[8 + fg, wide + j]
        ar, ai = con[pl.ds(h0 + i, 1), :], con[pl.ds(h0 + pc * parts + i, 1), :]
        er, ei = ar * pr - ai * pi, ar * pi + ai * pr
        lr, lm = con[f0 : f0 + 16, :], con[f0 + 16 : f0 + 32, :]
        at = pl.multiple_of(j * window + ki * 16, 16)
        t2[pl.ds(at, 16), :] = (lr * er - lm * ei).astype(BF)
        t2[pl.ds(pl.multiple_of(half + at, 16), 16), :] = (lr * ei + lm * er).astype(BF)
        return carry

    lax.fori_loop(0, pc * parts, row_body, 0)

    def part_product(src, block):
        start = pl.multiple_of(src * rows, rows)
        return jnp.dot(t2[:, pl.ds(start, rows)], block, preferred_element_type=F32)

    acc = part_product(c, s_send[c])
    for step in col_steps[::-1]:
        src = col_at(step, -1)
        col_link(s_send, s_recv, sa, ra, src, src).wait_recv()
        acc += part_product(src, s_recv[src])
    win = (acc[:half] + spin(acc[half:], -1.0, 1.0)).astype(BF)
    for j in range(pc):
        g_send[j] = win[j * window : (j + 1) * window]

    def each_facet(q, act):
        pair = pair_at(q)
        for g in range(groups):
            for h in range(2):
                index = g * 8 + 2 * pair + h
                if q == 0:
                    pl.when(index != f)(functools.partial(act, index))
                else:
                    act(index)

    def send_window(index):
        facet_link(g_send, g_recv, sb, rb, index, f).start()

    def take_window(index):
        facet_link(g_send, g_recv, sb, rb, index, index).wait_recv()

    def send_back(index):
        facet_link(r_send, r_recv, sc, rc, index, f).start()

    def take_back(index):
        facet_link(r_send, r_recv, sc, rc, index, index).wait_recv()

    far_first = (2, 3, 1, 0)
    for q in far_first:
        each_facet(q, send_window)
    g_recv[f] = g_send[f]

    first = cells[0, pl.ds(f, 1), :]
    second = cells[1, pl.ds(f, 1), :]

    def wave(count, step, cell):
        index = step * lax.broadcasted_iota(jnp.int32, (count, vis), 0)
        angle = (index * cell & (S - 1)).astype(F32) * (-2.0 * math.pi / S)
        return jnp.cos(angle), jnp.sin(angle)

    l0r, l0i = wave(16, 1, first)
    l1r, l1i = wave(max(groups * parts, 8), 16, first)
    for i in range(groups * parts):
        er, ei = l1r[i : i + 1], l1i[i : i + 1]
        g, k = i // parts, i % parts
        at = g * two + k * 16
        lt[at : at + 16, :] = (l0r * er - l0i * ei).astype(BF)
        lt[at + window : at + window + 16, :] = (l0r * ei + l0i * er).astype(BF)
    m0r, m0i = wave(16, 1, second)
    r1r[...], r1i[...] = wave(S // 16, 16, second)

    def right_body(i, carry):
        er, ei = r1r[pl.ds(i, 1), :], r1i[pl.ds(i, 1), :]
        at = pl.multiple_of(i * 16, 16)
        rtr[pl.ds(at, 16), :] = m0r * er - m0i * ei
        rti[pl.ds(at, 16), :] = m0r * ei + m0i * er
        return carry

    lax.fori_loop(0, S // 16, right_body, 0)

    pred_r = jnp.zeros((8, vis), F32)
    pred_i = jnp.zeros((8, vis), F32)
    for q in far_first[::-1]:
        each_facet(q, take_window)
        for h in range(2):
            b = 2 * pair_at(q) + h
            inner = None
            for g in range(groups):
                block = g_recv[g * 8 + b].astype(F32)
                both = jnp.concatenate([block, spin(block, -1.0, 1.0)], axis=0)
                term = jnp.dot(
                    both.T.astype(BF), lt[g * two : (g + 1) * two, :], preferred_element_type=F32
                )
                inner = term if inner is None else inner + term
            ir, ii = inner[:window], inner[window:]
            at = pl.multiple_of(b * window, window)
            rr, ri = rtr[pl.ds(at, window), :], rti[pl.ds(at, window), :]
            pred_r += jnp.sum((ir * rr - ii * ri).reshape(window // 8, 8, vis), axis=0)
            pred_i += jnp.sum((ir * ri + ii * rr).reshape(window // 8, 8, vis), axis=0)
    live = lax.broadcasted_iota(jnp.int32, (1, vis), 1) < counts[f]
    res_r = jnp.where(
        live, obs[0, pl.ds(f, 1), :] - jnp.sum(pred_r, axis=0, keepdims=True) / S, 0.0
    )
    res_i = jnp.where(
        live, obs[1, pl.ds(f, 1), :] - jnp.sum(pred_i, axis=0, keepdims=True) / S, 0.0
    )

    scale = 1.0 / math.sqrt(vis)
    for n, q in enumerate(far_first):
        base = n * 2 * two
        for h in range(2):
            at = pl.multiple_of((2 * pair_at(q) + h) * window, window)
            rr, ri = rtr[pl.ds(at, window), :], rti[pl.ds(at, window), :]
            low = base + h * two
            wt[low : low + window, :] = (res_r * rr + res_i * ri).astype(BF)
            wt[low + window : low + two, :] = (res_i * rr - res_r * ri).astype(BF)
        grid = lax.dot_general(
            lt[...], wt[base : base + 2 * two, :], nt, preferred_element_type=F32
        )
        for g in range(groups):
            for h in range(2):
                u = grid[g * two : g * two + window, h * two : (h + 1) * two]
                v = grid[g * two + window : (g + 1) * two, h * two : (h + 1) * two]
                index = g * 8 + 2 * pair_at(q) + h
                r_send[index] = ((u + spin(v, 1.0, -1.0)) * scale).astype(BF)
        each_facet(q, send_back)
    r_recv[f] = r_send[f]
    for i in range(2 * half // 256):
        tt[:, i * 256 : (i + 1) * 256] = t2[i * 256 : (i + 1) * 256, :].T
    for q in far_first[::-1]:
        each_facet(q, take_back)

    ret = r_recv[...].reshape(half, two)
    other = spin(ret.astype(F32), 1.0, -1.0).astype(BF)

    def back_strip(cp):
        at = pl.multiple_of(cp * rows, rows)
        strip = jnp.dot(tt[pl.ds(at, rows), :half], ret, preferred_element_type=F32)
        strip += jnp.dot(tt[pl.ds(at, rows), half:], other, preferred_element_type=F32)
        b_send[cp] = strip.astype(BF)

    for step in col_steps:
        peer = col_at(step, 1)
        back_strip(peer)
        col_link(b_send, b_recv, sd, rd, peer, c).start()
    back_strip(c)
    back_out[c] = b_send[c]
    for step in col_steps[::-1]:
        src = col_at(step, -1)
        col_link(b_send, b_recv, sd, rd, src, src).wait_recv()
        back_out[src] = b_recv[src]
    for step in col_steps:
        peer = col_at(step, 1)
        col_link(s_send, s_recv, sa, ra, peer, c).wait_send()
        col_link(b_send, b_recv, sd, rd, peer, c).wait_send()
    for d in range(1, nf):
        peer = lax.rem(f + d, nf)
        facet_link(g_send, g_recv, sb, rb, peer, f).wait_send()
        facet_link(r_send, r_recv, sc, rc, peer, f).wait_send()


def image_kernel(nc, back, tab, out, buf, sem):
    tiles, tile = buf.shape[0], buf.shape[3]
    strip = jnp.concatenate([back[k] for k in range(nc)], axis=1)
    stores = []
    for t in range(tiles):
        for part in range(2):
            piece = tab[part, :, t * tile : (t + 1) * tile]
            buf[t, part] = jnp.dot(strip, piece, preferred_element_type=F32)
        store = pltpu.make_async_copy(
            buf.at[t], out.at[:, :, t * tile : (t + 1) * tile], sem.at[t]
        )
        store.start()
        stores.append(store)
    for store in stores:
        store.wait()


def solution(mesh):
    nf, nc = mesh.shape["facet"], mesh.shape["col"]

    def on_device(facets, observed, uv_cells, counts):
        rows, extent = facets.shape[1:]
        vis = observed.shape[2]
        pc = counts.shape[0]
        window = S // 8
        two = 2 * window
        groups = nf // 8
        assert pc == nf and nf % 8 == 0 and nf <= 32
        con, scal = make_constants(nf, nc, pc, extent)
        vmem = pl.BlockSpec(memory_space=pltpu.VMEM)
        smem = pl.BlockSpec(memory_space=pltpu.SMEM)
        hbm = pl.BlockSpec(memory_space=pltpu.HBM)
        dma = pltpu.SemaphoreType.DMA
        back, tab = pl.pallas_call(
            functools.partial(cycle_kernel, nf, nc),
            out_shape=(
                jax.ShapeDtypeStruct((nc, rows, two), BF),
                jax.ShapeDtypeStruct((2, nc * two, extent), BF),
            ),
            in_specs=[vmem, vmem, vmem, smem, vmem, smem],
            out_specs=(vmem, vmem),
            scratch_shapes=[
                pltpu.VMEM((2 * pc * window, extent), BF),
                pltpu.VMEM((extent, 2 * pc * window), BF),
                pltpu.VMEM((nc, rows, two), BF),
                pltpu.VMEM((nc, rows, two), BF),
                pltpu.VMEM((pc, window, two), BF),
                pltpu.VMEM((nf, window, two), BF),
                pltpu.VMEM((groups * two, vis), BF),
                pltpu.VMEM((S, vis), F32),
                pltpu.VMEM((S, vis), F32),
                pltpu.VMEM((S // 16, vis), F32),
                pltpu.VMEM((S // 16, vis), F32),
                pltpu.VMEM((2 * S, vis), BF),
                pltpu.VMEM((nf, window, two), BF),
                pltpu.VMEM((pc, window, two), BF),
                pltpu.VMEM((nc, rows, two), BF),
                pltpu.VMEM((nc, rows, two), BF),
                dma((nc,)), dma((nc,)), dma((nf,)), dma((nf,)),
                dma((nf,)), dma((nf,)), dma((nc,)), dma((nc,)),
            ],
            compiler_params=pltpu.CompilerParams(
                collective_id=0, has_side_effects=True, vmem_limit_bytes=44 * 2**20
            ),
            name="cycle",
        )(facets, observed, uv_cells, counts, jnp.asarray(con), jnp.asarray(scal))
        tile = 256
        return pl.pallas_call(
            functools.partial(image_kernel, nc),
            out_shape=jax.ShapeDtypeStruct((2, rows, extent), F32),
            in_specs=[vmem, vmem],
            out_specs=hbm,
            scratch_shapes=[
                pltpu.VMEM((extent // tile, 2, rows, tile), F32),
                dma((extent // tile,)),
            ],
            compiler_params=pltpu.CompilerParams(vmem_limit_bytes=16 * 2**20),
            name="image",
        )(back, tab)

    return jax.shard_map(
        on_device,
        mesh=mesh,
        in_specs=(
            P(None, ("facet", "col"), None),
            P(None, "col", None),
            P(None, "col", None),
            P("col"),
        ),
        out_specs=P(None, ("facet", "col"), None),
        check_vma=False,
    )
```

time: 35.3 us -> 35.3 us (level)
  Pallas kernels: 35.1 us -> 29.6 us
  local copies, waits for them, and re-layouts: 0 us -> 5.34 us
    unnamed x0 -> x12, local copies, waits for them, and re-layouts: none -> 5.34 us
    pallas_call x1, Pallas kernels: 30.7 us -> 27.9 us  [on_device(): pl.pallas_call(functools.partial(cycle_kernel, nf, nc), out_shape=(jax.Sh...]
    pallas_call x1, Pallas kernels: 4.4 us -> 1.66 us  [on_device(): pl.pallas_call(functools.partial(image_kernel, nc), out_shape=jax.ShapeDt...]
where the time goes in v1:
time: 35.3 us; the launch traced here: 34.9 us
  Pallas kernels  29.6 us (84%)
  local copies, waits for them, and re-layouts  5.34 us (15%)
    pallas_call x1, Pallas kernels, on_device(): pl.pallas_call(functools.partial(cycle_kernel, nf, nc), out_shape=(jax.Sh...  27.9 us
    unnamed x12, local copies, waits for them, and re-layouts  5.34 us
    pallas_call x1, Pallas kernels, on_device(): pl.pallas_call(functools.partial(image_kernel, nc), out_shape=jax.ShapeDt...  1.66 us

profile of v1, /device:TPU:0, one launch (start us, length us, event | category | flops | bytes accessed | tf_op | source)
XLA Modules:
  0.0 34.9 jit_solution(2195773787653967267)
XLA Ops:
  0.0 0.0 copy-start
  0.0 1.2 %copy-done = bf16[2,256,1024]{2,1,0:T(8,128)(2,1)S(1)} copy-done((bf16[2,256,1024]{2,1,0:T(8,128)(2,1)S(1)}, bf16[2,256,1024]{2,1,0:T(8,128)(2,1)}, u32[]{:S(2)}) %copy-start) | copy-done | bytes 1048600
  1.2 0.0 copy-start.1
  1.2 1.1 %copy-done.1 = f32[160,1024]{1,0:T(8,128)S(1)} copy-done((f32[160,1024]{1,0:T(8,128)S(1)}, f32[160,1024]{1,0:T(8,128)}, u32[]{:S(2)}) %copy-start.1) | copy-done | bytes 655384
  2.3 0.0 copy-start.2
  2.3 0.8 %copy-done.2 = f32[2,8,1024]{2,1,0:T(8,128)S(1)} copy-done((f32[2,8,1024]{2,1,0:T(8,128)S(1)}, f32[2,8,1024]{2,1,0:T(8,128)}, u32[]{:S(2)}) %copy-start.2) | copy-done | bytes 65560
  3.2 0.0 copy-start.3
  3.2 0.8 %copy-done.3 = s32[2,8,1024]{2,1,0:T(8,128)S(1)} copy-done((s32[2,8,1024]{2,1,0:T(8,128)S(1)}, s32[2,8,1024]{2,1,0:T(8,128)}, u32[]{:S(2)}) %copy-start.3) | copy-done | bytes 65560
  4.0 0.0 copy-start.4
  4.0 0.7 %copy-done.4 = f32[9,16]{1,0:T(8,128)S(1)} copy-done((f32[9,16]{1,0:T(8,128)S(1)}, f32[9,16]{1,0:T(8,128)}, u32[]{:S(2)}) %copy-start.4) | copy-done | bytes 600
  4.7 0.0 copy-start.5
  4.7 0.7 %copy-done.5 = s32[8]{0:T(128)S(1)} copy-done((s32[8]{0:T(128)S(1)}, s32[8]{0:T(128)}, u32[]{:S(2)}) %copy-start.5) | copy-done | bytes 56
  5.3 27.9 %cycle.1 = (bf16[4,256,128]{2,1,0:T(8,128)(2,1)S(1)}, bf16[2,512,1024]{2,1,0:T(8,128)(2,1)S(1)}) custom-call(bf16[2,256,1024]{2,1,0:T(8,128)(2,1)S(1)} %copy-done, f32[2,8,1024]{2,1,0:T(8,128)S(1)} %copy-done.2, s32[2,8,1024]{2,1,0:T(8,128)S(1)} %copy-done.3, s32[8]{0:T(128)S(1)} %copy-done.5, f32[160,1024]{1,0:T(8,128)S(1)} %copy-done.1, f32[9,16]{1,0:T(8,128)S(1)} %copy-done.4), custom_call_target="tpu_custom_call" | custom-call | tf_op jit(solution)/shard_map/cycle/pallas_call | solution.py:349
  33.3 1.7 %image.1 = f32[2,256,1024]{2,1,0:T(8,128)} custom-call(bf16[4,256,128]{2,1,0:T(8,128)(2,1)S(1)} %get-tuple-element.7.back, bf16[2,512,1024]{2,1,0:T(8,128)(2,1)S(1)} %get-tuple-element.8.tab), custom_call_target="tpu_custom_call" | custom-call | tf_op jit(solution)/shard_map/image/pallas_call | solution.py:383
Async XLA Ops:
  0.0 1.2 %copy-start = (bf16[2,256,1024]{2,1,0:T(8,128)(2,1)S(1)}, bf16[2,256,1024]{2,1,0:T(8,128)(2,1)}, u32[]{:S(2)}) copy-start(bf16[2,256,1024]{2,1,0:T(8,128)(2,1)} %xbuf.1) | copy-start | bytes 3145732
  1.2 1.1 %copy-start.1 = (f32[160,1024]{1,0:T(8,128)S(1)}, f32[160,1024]{1,0:T(8,128)}, u32[]{:S(2)}) copy-start(f32[160,1024]{1,0:T(8,128)} %constant.4.clone.con) | copy-start | bytes 1966084
  2.3 0.8 %copy-start.2 = (f32[2,8,1024]{2,1,0:T(8,128)S(1)}, f32[2,8,1024]{2,1,0:T(8,128)}, u32[]{:S(2)}) copy-start(f32[2,8,1024]{2,1,0:T(8,128)} %obs.1) | copy-start | bytes 196612
  3.2 0.8 %copy-start.3 = (s32[2,8,1024]{2,1,0:T(8,128)S(1)}, s32[2,8,1024]{2,1,0:T(8,128)}, u32[]{:S(2)}) copy-start(s32[2,8,1024]{2,1,0:T(8,128)} %cells.1) | copy-start | bytes 196612
  4.0 0.7 %copy-start.4 = (f32[9,16]{1,0:T(8,128)S(1)}, f32[9,16]{1,0:T(8,128)}, u32[]{:S(2)}) copy-start(f32[9,16]{1,0:T(8,128)} %constant.5.clone.scal) | copy-start | bytes 1732
  4.7 0.7 %copy-start.5 = (s32[8]{0:T(128)S(1)}, s32[8]{0:T(128)}, u32[]{:S(2)}) copy-start(s32[8]{0:T(128)} %counts.1) | copy-start | bytes 100

commit v2 on v1

--- a/solution.py
+++ b/solution.py
@@ -64,10 +64,10 @@
 
 
 def cycle_kernel(
-    nf, nc, xbuf, obs, cells, counts, con, scal, back_out, tab,
-    t2, tt, s_send, s_recv, g_send, g_recv, lt, rtr, rti, r1r, r1i, wt,
+    nf, nc, x_hbm, obs_hbm, cells_hbm, counts, con_hbm, scal, back_out, tab,
+    xbuf, obs, cells, con, t2, tt, s_send, s_recv, g_send, g_recv, lt, rtr, rti, r1r, r1i, wt,
     r_send, r_recv, b_send, b_recv,
-    sa, ra, sb, rb, sc, rc, sd, rd,
+    in_sem, sa, ra, sb, rb, sc, rc, sd, rd,
 ):
     f = lax.axis_index("facet")
     c = lax.axis_index("col")
@@ -112,6 +112,16 @@
     e1 = 32
     f0 = e1 + 2 * nc * parts
     h0 = f0 + 32
+    last = con.shape[0]
+    loads = [
+        pltpu.make_async_copy(con_hbm.at[0:f0], con.at[0:f0], in_sem.at[0]),
+        pltpu.make_async_copy(x_hbm, xbuf, in_sem.at[1]),
+        pltpu.make_async_copy(con_hbm.at[f0:last], con.at[f0:last], in_sem.at[2]),
+        pltpu.make_async_copy(obs_hbm, obs, in_sem.at[3]),
+        pltpu.make_async_copy(cells_hbm, cells, in_sem.at[4]),
+    ]
+    for load in loads:
+        load.start()
     nt = (((1,), (1,)), ((), ()))
     fm = lax.rem(f, 8)
 
@@ -137,9 +147,12 @@
         strip += lax.dot_general(xbuf[1], tab[1, pl.ds(at, two), :], nt, preferred_element_type=F32)
         s_send[cp] = strip.astype(BF)
 
+    loads[0].wait()
     for n, step in enumerate(col_steps):
         peer = col_at(step, 1)
         column_table(peer)
+        if n == 0:
+            loads[1].wait()
         column_strip(peer)
         if n == 0:
             pl.semaphore_wait(barrier, nc - 1 + nf - 1)
@@ -149,6 +162,8 @@
 
     half = pc * window
     fg = f // 8
+
+    loads[2].wait()
 
     def row_body(i, carry):
         j = i // parts
@@ -204,6 +219,8 @@
         each_facet(q, send_window)
     g_recv[f] = g_send[f]
 
+    loads[3].wait()
+    loads[4].wait()
     first = cells[0, pl.ds(f, 1), :]
     second = cells[1, pl.ds(f, 1), :]
 
@@ -346,15 +363,20 @@
         smem = pl.BlockSpec(memory_space=pltpu.SMEM)
         hbm = pl.BlockSpec(memory_space=pltpu.HBM)
         dma = pltpu.SemaphoreType.DMA
+        fixed = functools.partial(pltpu.with_memory_space_constraint, memory_space=pltpu.HBM)
         back, tab = pl.pallas_call(
             functools.partial(cycle_kernel, nf, nc),
             out_shape=(
                 jax.ShapeDtypeStruct((nc, rows, two), BF),
                 jax.ShapeDtypeStruct((2, nc * two, extent), BF),
             ),
-            in_specs=[vmem, vmem, vmem, smem, vmem, smem],
+            in_specs=[hbm, hbm, hbm, smem, hbm, smem],
             out_specs=(vmem, vmem),
             scratch_shapes=[
+                pltpu.VMEM((2, rows, extent), BF),
+                pltpu.VMEM((2, pc, vis), F32),
+                pltpu.VMEM((2, pc, vis), jnp.int32),
+                pltpu.VMEM(con.shape, F32),
                 pltpu.VMEM((2 * pc * window, extent), BF),
                 pltpu.VMEM((extent, 2 * pc * window), BF),
                 pltpu.VMEM((nc, rows, two), BF),
@@ -371,6 +393,7 @@
                 pltpu.VMEM((pc, window, two), BF),
                 pltpu.VMEM((nc, rows, two), BF),
                 pltpu.VMEM((nc, rows, two), BF),
+                dma((5,)),
                 dma((nc,)), dma((nc,)), dma((nf,)), dma((nf,)),
                 dma((nf,)), dma((nf,)), dma((nc,)), dma((nc,)),
             ],
@@ -378,7 +401,10 @@
                 collective_id=0, has_side_effects=True, vmem_limit_bytes=44 * 2**20
             ),
             name="cycle",
-        )(facets, observed, uv_cells, counts, jnp.asarray(con), jnp.asarray(scal))
+        )(
+            fixed(facets), fixed(observed), fixed(uv_cells), fixed(counts),
+            fixed(jnp.asarray(con)), fixed(jnp.asarray(scal)),
+        )
         tile = 256
         return pl.pallas_call(
             functools.partial(image_kernel, nc),

time: 35.3 us -> 30 us (0.85)
  local copies, waits for them, and re-layouts: 5.34 us -> 0 us
    unnamed x12 -> x0, local copies, waits for them, and re-layouts: 5.34 us -> none
where the time goes in v2:
time: 30 us; the launch traced here: 29.7 us
  Pallas kernels  29.7 us (99%)
    pallas_call x1, Pallas kernels, on_device(): pl.pallas_call(functools.partial(cycle_kernel, nf, nc), out_shape=(jax.Sh...  28.1 us
    pallas_call x1, Pallas kernels, on_device(): pl.pallas_call(functools.partial(image_kernel, nc), out_shape=jax.ShapeDt...  1.65 us

profile of v2, /device:TPU:0, one launch (start us, length us, event | category | flops | bytes accessed | tf_op | source)
XLA Modules:
  0.0 29.7 jit_solution(1708407171216576237)
XLA Ops:
  0.0 28.1 %cycle.1 = (bf16[4,256,128]{2,1,0:T(8,128)(2,1)S(1)}, bf16[2,512,1024]{2,1,0:T(8,128)(2,1)S(1)}) custom-call(bf16[2,256,1024]{2,1,0:T(8,128)(2,1)} %x_hbm.1, f32[2,8,1024]{2,1,0:T(8,128)} %obs_hbm.1, s32[2,8,1024]{2,1,0:T(8,128)} %cells_hbm.1, s32[8]{0:T(128)} %counts.1, f32[160,1024]{1,0:T(8,128)} %constant.4.clone.con_hbm, f32[9,16]{1,0:T(8,128)} %constant.5.clone.scal), custom_call_target="tpu_custom_call" | custom-call | tf_op jit(solution)/shard_map/cycle/pallas_call | solution.py:367
  28.1 1.7 %image.1 = f32[2,256,1024]{2,1,0:T(8,128)} custom-call(bf16[4,256,128]{2,1,0:T(8,128)(2,1)S(1)} %get-tuple-element.7.back, bf16[2,512,1024]{2,1,0:T(8,128)(2,1)S(1)} %get-tuple-element.8.tab), custom_call_target="tpu_custom_call" | custom-call | tf_op jit(solution)/shard_map/image/pallas_call | solution.py:409
